TPU v7x, 128 devices: a whole 4x4x4 slice. The times are simulated.
128 devices in a mesh: rows: 32 (over x, z_hi, y), cols: 4 (over z_lo, core).
Axes of the slice: x: 4, y: 4, z: 4 (z_hi: 2, z_lo: 2; z = z_hi * 2 + z_lo), core: 2. Of those that a mesh axis runs over, the one named last changes fastest.
Arguments:
- mantissa: bfloat16 [8192, 8192], P('rows', 'cols'), may hold values from 0.5 to 1
- exponents: int32 [512, 64], P('rows'), may hold values from -3 to 1
Outputs:
- spectrum_real: float32 [8192, 8192], P(('rows', 'cols'))
- spectrum_imag: float32 [8192, 8192], P(('rows', 'cols'))
Inputs may be any that keep to these rules, and one draw needn't show every extreme that they name: `exponents`: each entry scales its block of 16 rows and 128 columns of the table by 2 to that power.
All inputs are finite; a program needn't handle non-finite values.
Results may differ from a plain program's by a relative error of at most 0.0013.
Values may be sent and summed in bfloat16 or wider, within the bound.
A program may use at most 64 MiB of HBM per device.

v0:
```python
import math

import jax
import jax.numpy as jnp
import ml_dtypes
import numpy as np
from jax import lax
from jax.experimental import pallas as pl
from jax.experimental.pallas import tpu as pltpu
from jax.sharding import PartitionSpec as P

NR = 8192
NC = 8192
MESH = pl.DeviceIdType.MESH
CHUNKS = 8
LAG = 2
TOP = 32767.0
BOUND = 16896.0
F32 = jnp.float32
BF16 = jnp.bfloat16


def halves(table):
    high = table.astype(ml_dtypes.bfloat16)
    low = (table - high.astype(np.float64)).astype(ml_dtypes.bfloat16)
    return np.stack([high, low])


def send_table():
    sides = []
    for side in range(2):
        t = np.arange(64)
        row, core = t // 2, t % 2
        z_lo = ((row // 4) % 2 + side) % 2
        a = 4 * row + 2 * z_lo + core
        jo = np.arange(128)[:, None]
        one = 2 * np.pi * (jo * a % 128) / 128
        two = 2 * np.pi * (jo * (a + 1) % 128) / 128
        from_re = np.concatenate([np.cos(one), -np.sin(one), np.cos(two), -np.sin(two)], 1)
        from_im = np.concatenate([np.sin(one), np.cos(one), -np.sin(two), -np.cos(two)], 1)
        sides.append(halves(np.concatenate([from_re, from_im], 0)))
    return np.stack(sides)


def receive_table():
    k0 = np.arange(128)[None, :]
    blocks = []
    for half in range(2):
        s = 2 * np.arange(64)[:, None] + half
        angle = 2 * np.pi * (s * k0 % 128) / 128
        blocks.append(np.concatenate([np.cos(angle), -np.sin(angle)], 1))
        blocks.append(np.concatenate([np.sin(angle), np.cos(angle)], 1))
    return halves(np.concatenate(blocks, 0))


def twist_table(count, scale):
    angle = 2 * np.pi * (np.arange(count)[:, None] * np.arange(128)[None, :]) / 8192
    table = np.stack([np.cos(angle), -np.sin(angle)], 1).reshape(2 * count, 128) * scale
    return table.astype(np.float32)


def c_add(u, v):
    im = v[1] if u[1] is None else (u[1] if v[1] is None else u[1] + v[1])
    return (u[0] + v[0], im)


def c_sub(u, v):
    im = (None if v[1] is None else -v[1]) if u[1] is None else (u[1] if v[1] is None else u[1] - v[1])
    return (u[0] - v[0], im)


def sub_i(u, v):
    re = u[0] if v[1] is None else u[0] + v[1]
    return (re, -v[0] if u[1] is None else u[1] - v[0])


def add_i(u, v):
    re = u[0] if v[1] is None else u[0] - v[1]
    return (re, v[0] if u[1] is None else u[1] + v[0])


def c_scale(u, cos, sin):
    if u[1] is None:
        return (u[0] * cos, u[0] * (-sin))
    return (u[0] * cos + u[1] * sin, u[1] * cos - u[0] * sin)


ROOT = math.sqrt(0.5)


def dft4(x):
    t0, t1 = c_add(x[0], x[2]), c_sub(x[0], x[2])
    t2, t3 = c_add(x[1], x[3]), c_sub(x[1], x[3])
    return [c_add(t0, t2), sub_i(t1, t3), c_sub(t0, t2), add_i(t1, t3)]


def dft8(x, half=False):
    even, odd = dft4(x[0::2]), dft4(x[1::2])
    o1, o3 = odd[1], odd[3]
    w1 = ((o1[0] + o1[1]) * ROOT, (o1[1] - o1[0]) * ROOT)
    y = [c_add(even[0], odd[0]), c_add(even[1], w1), sub_i(even[2], odd[2]), None, c_sub(even[0], odd[0])]
    w3 = ((o3[1] - o3[0]) * ROOT, (o3[0] + o3[1]) * -ROOT)
    y[3] = c_add(even[3], w3)
    if half:
        return y
    return y + [c_sub(even[1], w1), add_i(even[2], odd[2]), c_sub(even[3], w3)]


def twist64(u, n):
    n = n % 64
    if n == 0:
        return u
    return c_scale(u, math.cos(2 * math.pi * n / 64), math.sin(2 * math.pi * n / 64))


def code(x):
    u = lax.rsqrt(lax.rsqrt(jnp.maximum(jnp.abs(x) * (1.0 / BOUND), 1e-30)))
    n = (u * TOP + 0.5).astype(jnp.int32)
    return jnp.where(x < 0, -n, n)


def decode(n):
    v = n.astype(F32)
    return (v * jnp.abs(v)) * (v * v)


DECODED = BOUND / TOP**4


def split(x):
    high = x.astype(BF16)
    return high, (x - high.astype(F32)).astype(BF16)


def exchange(
    mant, exps_in, send_w, recv_w, send_t, recv_t,
    z_out,
    block, masses, first, a_hi, a_lo, products, words, outbox, inbox, b_hi, b_lo, result,
    exps, w_ref, e_ref, t1_ref, t2_ref, edge_in, edge, above, last, last_in,
    s_blk, r_blk, s_out, r_out, s_edge, r_edge, s_last, r_last, tab_sem, edge_sem, z_sem, exp_sem, sem_b, sem_c, sem_d,
):
    row, col = lax.axis_index("rows"), lax.axis_index("cols")
    x, z_hi, y = row // 8, (row // 4) % 2, row % 4
    z_lo, core = col // 2, col % 2
    side = (z_hi + z_lo) % 2
    me = row * 2 + core
    my_cols = pl.ds(pl.multiple_of(2048 * col, 2048), 2048)

    def at(r, c):
        return dict(device_id={"rows": r, "cols": c}, device_id_type=MESH)

    def mate(m):
        other = (core + m % 2) % 2
        return ((z_lo + m // 2) % 2) * 2 + other, other

    tables = (
        pltpu.make_async_copy(send_w.at[side], w_ref, tab_sem.at[0]),
        pltpu.make_async_copy(recv_w, e_ref, tab_sem.at[1]),
        pltpu.make_async_copy(send_t, t1_ref, tab_sem.at[2]),
        pltpu.make_async_copy(recv_t, t2_ref, tab_sem.at[3]),
    )
    edges = (
        pltpu.make_async_copy(mant.at[:, 0], edge_in.at[0], edge_sem.at[0]),
        pltpu.make_async_copy(mant.at[:, 7], edge_in.at[1], edge_sem.at[1]),
    )
    exp_copy = pltpu.make_async_copy(exps_in, exps, exp_sem)
    exp_copy.start()
    for copy in edges + tables:
        copy.start()

    barrier = pltpu.get_barrier_semaphore()
    count = 0
    for m in (1, 2, 3):
        pl.semaphore_signal(barrier, inc=1, **at(row, mate(m)[0]))
        count += 1
    for other in (core, 1 - core):
        pl.semaphore_signal(barrier, inc=1, **at(x * 8 + (1 - z_hi) * 4 + y, (1 - z_lo) * 2 + other))
        count += 1
    for d in (1, 2, 3):
        pl.semaphore_signal(barrier, inc=1, **at(x * 8 + z_hi * 4 + (y + d) % 4, col))
        pl.semaphore_signal(barrier, inc=1, **at((x + d) % 4 * 8 + z_hi * 4 + y, col))
        count += 2

    exp_copy.wait()
    for copy in edges:
        copy.wait()
    for g in range(4):
        for j in range(16):
            lanes = slice(128 * j, 128 * (j + 1))
            e = exps[4 * g, 16 * col + j]
            scale = jnp.left_shift(1, e + 3).astype(F32) * 0.125
            edge[g // 2, g % 2 : g % 2 + 1, lanes] = edge_in[0, g, :, lanes].astype(F32)[7:8] * scale
            if g % 2:
                e = exps[4 * g + 3, 16 * col + j]
                scale = jnp.left_shift(1, e + 3).astype(F32) * 0.125
                last[g // 2, :, lanes] = edge_in[1, g, :, lanes].astype(F32)[7:8] * scale

    pl.semaphore_wait(barrier, count)
    for m in (1, 2, 3):
        c, other = mate(m)
        pltpu.make_async_remote_copy(
            edge.at[other], above.at[:, my_cols], s_edge, r_edge, **at(row, c)
        ).start()
    pltpu.make_async_copy(edge.at[core], above.at[:, my_cols], r_edge).start()

    def send_block(q):
        for m in (2, 3, 1):
            c, other = mate(m)
            pltpu.make_async_remote_copy(
                mant.at[pl.ds(2 * other, 2), q], block.at[:, q, :, my_cols], s_blk.at[q], r_blk.at[q], **at(row, c)
            ).start()
        pltpu.make_async_copy(
            mant.at[pl.ds(2 * core, 2), q], block.at[:, q, :, my_cols], r_blk.at[q]
        ).start()

    @pl.loop(0, CHUNKS)
    def _(j):
        send_block((j + 1) % CHUNKS)

    for d in (1, 2, 3):
        pl.semaphore_signal(sem_b, inc=1, **at(x * 8 + z_hi * 4 + (y + d) % 4, col))
    pl.semaphore_wait(sem_b, 3)
    for d in (1, 2, 3):
        pl.semaphore_signal(sem_c, inc=1, **at((x + d) % 4 * 8 + z_hi * 4 + y, col))

    for copy in tables:
        copy.wait()
    ref = above
    pltpu.make_async_copy(ref, ref, r_edge).wait()
    sub8 = lax.broadcasted_iota(jnp.int32, (8, 128), 0)
    lane8 = lax.broadcasted_iota(jnp.int32, (8, 128), 1)

    pl.semaphore_wait(sem_c, 3)
    pl.semaphore_signal(sem_d, inc=1, **at(x * 8 + (1 - z_hi) * 4 + y, (1 - z_lo) * 2 + core))

    def send_last():
        pl.semaphore_wait(sem_d, 1)
        for m in (1, 2, 3):
            c, other = mate(m)
            pltpu.make_async_remote_copy(
                last.at[1 - other], last_in.at[:, my_cols], s_last, r_last, **at((row + 1 - other) % 32, c)
            ).start()

        @pl.when(core == 1)
        def _():
            pltpu.make_async_copy(last.at[0], last_in.at[:, my_cols], r_last).start()

        @pl.when(core == 0)
        def _():
            pltpu.make_async_remote_copy(
                last.at[1], last_in.at[:, my_cols], s_last, r_last, **at((row + 1) % 32, col)
            ).start()

    def send_phase(q):
        ref = block.at[:, q]
        pltpu.make_async_copy(ref, ref, r_blk.at[q]).wait()

        for h in range(2):
            before = None
            for c in range(64):
                lanes = slice(128 * c, 128 * (c + 1))
                e = exps[8 * core + 4 * h + q // 2, c]
                scale = jnp.left_shift(1, e + 3).astype(F32) * 0.125
                here = block[h, q, :, lanes].astype(F32) * scale
                top = jnp.broadcast_to(above[h : h + 1, lanes], (8, 128))
                upper = jnp.where(sub8 == 0, top, pltpu.roll(here, 1, 0))
                above[h : h + 1, lanes] = here[7:8]
                step = here - upper
                rolled = pltpu.roll(step, 1, 1)
                left = jnp.where(lane8 == 0, 0.0 if before is None else before, rolled)
                before = rolled
                masses[c, 8 * h : 8 * h + 8, :] = step - left

        for c0 in range(8):
            spread = dft8([(masses[8 * c1 + c0], None) for c1 in range(8)], half=True)
            for b1 in range(5):
                value = twist64(spread[b1], c0 * b1)
                first[b1, c0, 0] = value[0]
                if value[1] is not None:
                    first[b1, c0, 1] = value[1]
        for b1 in range(5):
            real = b1 == 0
            spread = dft8(
                [
                    (first[b1, c0, 0], None if real or (b1 == 4 and c0 == 0) else first[b1, c0, 1])
                    for c0 in range(8)
                ],
                half=real,
            )
            for b0, (re, im) in enumerate(spread):
                b = b1 + 8 * b0
                if b1 == 4 and b0 >= 4:
                    continue
                if b > 32:
                    b, im = 64 - b, -im
                if b == 0:
                    tw_re, tw_im = re, jnp.zeros_like(re)
                else:
                    cos = jnp.broadcast_to(t1_ref[2 * b : 2 * b + 1, :], (16, 128))
                    sin = jnp.broadcast_to(t1_ref[2 * b + 1 : 2 * b + 2, :], (16, 128))
                    if im is None:
                        tw_re, tw_im = re * cos, re * sin
                    else:
                        tw_re, tw_im = re * cos - im * sin, re * sin + im * cos
                rows = slice(16 * b, 16 * b + 16)
                a_hi[rows, 0:128], a_lo[rows, 0:128] = split(tw_re)
                a_hi[rows, 128:256], a_lo[rows, 128:256] = split(tw_im)

        high = a_hi[...]
        products[...] = (
            jnp.dot(high, w_ref[0], preferred_element_type=F32)
            + jnp.dot(a_lo[...], w_ref[0], preferred_element_type=F32)
            + jnp.dot(high, w_ref[1], preferred_element_type=F32)
        )

        for b in range(33):
            for place, lanes in ((b, slice(0, 128)), (64 - b, slice(128, 256))):
                if b in (0, 32) and lanes.start:
                    continue
                low = code(products[16 * b : 16 * b + 8, lanes])
                top = code(products[16 * b + 8 : 16 * b + 16, lanes])
                words[8 * place : 8 * place + 8, :] = jnp.left_shift(top, 16) | (low & 0xFFFF)
        for p in range(4):
            tile = jnp.concatenate(
                [words[pl.ds(64 * g + i, 8, stride=8), :] for i in (2 * p, 2 * p + 1) for g in range(8)], 0
            )
            lanes = pl.ds(pl.multiple_of(512 * q + 128 * p, 128), 128)
            outbox[:, :, lanes] = tile.T.reshape(2, 64, 128)

        lanes = pl.ds(pl.multiple_of(512 * q, 512), 512)

        @pl.loop(1, 64)
        def _(m):
            flip, dc, dx, dy = m % 2, (m // 32) % 2, (m // 2) % 4, (m // 8) % 4
            to_hi, to_lo, to_core = (z_hi + flip) % 2, (z_lo + flip) % 2, (core + dc) % 2
            to_row = (x + dx) % 4 * 8 + to_hi * 4 + (y + dy) % 4
            pltpu.make_async_remote_copy(
                outbox.at[:, pl.ds(to_row * 2 + to_core, 1), lanes],
                inbox.at[:, pl.ds(me, 1), lanes],
                s_out.at[q],
                r_out.at[q],
                **at(to_row, to_lo * 2 + to_core),
            ).start()

        pltpu.make_async_copy(
            outbox.at[:, pl.ds(me, 1), lanes], inbox.at[:, pl.ds(me, 1), lanes], r_out.at[q]
        ).start()

    def receive_phase(q):
        lanes = pl.ds(pl.multiple_of(512 * q, 512), 512)
        ref = inbox.at[:, :, lanes]
        pltpu.make_async_copy(ref, ref, r_out.at[q]).wait()
        for p in range(4):
            lanes = pl.ds(pl.multiple_of(512 * q + 128 * p, 128), 128)
            tile = inbox[:, :, lanes].reshape(128, 128).T
            rows = slice(128 * p, 128 * p + 128)
            low = decode(jnp.right_shift(jnp.left_shift(tile, 16), 16))
            b_hi[rows, 0:128], b_lo[rows, 0:128] = split(low)
            top = decode(jnp.right_shift(tile, 16))
            b_hi[rows, 128:256], b_lo[rows, 128:256] = split(top)
        high = b_hi[...]
        value = (
            jnp.dot(high, e_ref[0], preferred_element_type=F32)
            + jnp.dot(b_lo[...], e_ref[0], preferred_element_type=F32)
            + jnp.dot(high, e_ref[1], preferred_element_type=F32)
        )
        for i in range(8):
            re, im = value[64 * i : 64 * i + 64, 0:128], value[64 * i : 64 * i + 64, 128:256]
            cos = t2_ref[pl.ds(16 * q + 2 * i, 1), :]
            sin = t2_ref[pl.ds(16 * q + 2 * i + 1, 1), :]
            result[8 * q + i, :, 0:128] = re * cos - im * sin
            result[8 * q + i, :, 128:256] = re * sin + im * cos
        ref = pl.ds(8 * q, 8)
        pltpu.make_async_copy(result.at[ref], z_out.at[ref], z_sem.at[q]).start()

    @pl.loop(0, CHUNKS + LAG)
    def _(j):
        @pl.when(j == CHUNKS - 1)
        def _():
            pltpu.make_async_copy(last_in, last_in, r_last).wait()
            above[1:2, :] = above[0:1, :]
            above[0:1, :] = jnp.where(row * 2 + core == 0, jnp.zeros_like(last_in[...]), last_in[...])

        @pl.when(j == 2)
        def _():
            send_last()

        @pl.when(j < CHUNKS)
        def _():
            send_phase((j + 1) % CHUNKS)

        @pl.when(j >= LAG)
        def _():
            receive_phase((j - LAG + 1) % CHUNKS)

    for m in (1, 2, 3):
        pltpu.make_async_copy(edge.at[0], edge.at[0], s_edge).wait()
    for q in range(CHUNKS):
        ref = block.at[:, q, :, pl.ds(0, 6144)]
        pltpu.make_async_copy(ref, ref, s_blk.at[q]).wait()
        ref = outbox.at[0, pl.ds(0, 24), pl.ds(0, 2688)]
        pltpu.make_async_copy(ref, ref, s_out.at[q]).wait()
        ref = pl.ds(8 * q, 8)
        pltpu.make_async_copy(result.at[ref], z_out.at[ref], z_sem.at[q]).wait()
    for m in (1, 2, 3):
        pltpu.make_async_copy(last.at[0], last.at[0], s_last).wait()

    @pl.when(core == 0)
    def _():
        pltpu.make_async_copy(last.at[0], last.at[0], s_last).wait()


def run_exchange(mantissa, exponents):
    dma = pltpu.SemaphoreType.DMA
    operands = (
        mantissa.reshape(4, 8, 8, 2048),
        exponents,
        jnp.asarray(send_table()),
        jnp.asarray(receive_table()),
        jnp.asarray(np.concatenate([twist_table(33, 1.0), np.zeros((6, 128), np.float32)])),
        jnp.asarray(twist_table(64, DECODED / math.sqrt(NR * NC))),
    )
    return pl.pallas_call(
        exchange,
        out_shape=jax.ShapeDtypeStruct((64, 64, 256), F32),
        in_specs=[pl.BlockSpec(memory_space=pltpu.HBM)] * 6,
        out_specs=pl.BlockSpec(memory_space=pl.ANY),
        scratch_shapes=[
            pltpu.VMEM((2, 8, 8, 8192), BF16),
            pltpu.VMEM((64, 16, 128), F32),
            pltpu.VMEM((5, 8, 2, 16, 128), F32),
            pltpu.VMEM((528, 256), BF16),
            pltpu.VMEM((528, 256), BF16),
            pltpu.VMEM((528, 256), F32),
            pltpu.VMEM((512, 128), jnp.int32),
            pltpu.VMEM((2, 64, 4096), jnp.int32),
            pltpu.VMEM((2, 64, 4096), jnp.int32),
            pltpu.VMEM((512, 256), BF16),
            pltpu.VMEM((512, 256), BF16),
            pltpu.VMEM((64, 64, 256), F32),
            pltpu.SMEM((16, 64), jnp.int32),
            pltpu.VMEM((2, 256, 256), BF16),
            pltpu.VMEM((2, 256, 256), BF16),
            pltpu.VMEM((72, 128), F32),
            pltpu.VMEM((128, 128), F32),
            pltpu.VMEM((2, 4, 8, 2048), BF16),
            pltpu.VMEM((2, 2, 2048), F32),
            pltpu.VMEM((2, 8192), F32),
            pltpu.VMEM((2, 1, 2048), F32),
            pltpu.VMEM((1, 8192), F32),
            dma((CHUNKS,)),
            dma((CHUNKS,)),
            dma((CHUNKS,)),
            dma((CHUNKS,)),
            dma,
            dma,
            dma,
            dma,
            dma((4,)),
            dma((2,)),
            dma((CHUNKS,)),
            dma,
            pltpu.SemaphoreType.REGULAR,
            pltpu.SemaphoreType.REGULAR,
            pltpu.SemaphoreType.REGULAR,
        ],
        compiler_params=pltpu.CompilerParams(
            collective_id=0, has_side_effects=True, vmem_limit_bytes=48 * 1024 * 1024
        ),
        name="exchange",
    )(*[pltpu.with_memory_space_constraint(operand, pltpu.HBM) for operand in operands])


def finish(z_ref, re_ref, im_ref, middle):
    for i0 in range(8):
        spread = dft8([(z_ref[8 * i1 + i0, :, 0:128], z_ref[8 * i1 + i0, :, 128:256]) for i1 in range(8)])
        for k_a in range(8):
            value = twist64(spread[k_a], i0 * k_a)
            middle[k_a, i0, 0] = value[0]
            middle[k_a, i0, 1] = value[1]
    for k_a in range(8):
        spread = dft8([(middle[k_a, i0, 0], middle[k_a, i0, 1]) for i0 in range(8)])
        for k_b, (re, im) in enumerate(spread):
            lanes = slice(128 * (k_a + 8 * k_b), 128 * (k_a + 8 * k_b + 1))
            re_ref[:, lanes] = re
            im_ref[:, lanes] = im


def run_finish(z):
    return pl.pallas_call(
        finish,
        grid=(8,),
        out_shape=[jax.ShapeDtypeStruct((64, NR), F32)] * 2,
        in_specs=[pl.BlockSpec((64, 8, 256), lambda g: (0, g, 0))],
        out_specs=[pl.BlockSpec((8, NR), lambda g: (g, 0))] * 2,
        scratch_shapes=[pltpu.VMEM((8, 8, 2, 8, 128), F32)],
        compiler_params=pltpu.CompilerParams(vmem_limit_bytes=48 * 1024 * 1024),
        name="finish",
    )(z)


def local(mantissa, exponents):
    re, im = run_finish(run_exchange(mantissa, exponents))
    return re, im


def solution(mesh):
    in_specs = (P("rows", "cols"), P("rows", None))
    out_specs = (P(("rows", "cols"), None), P(("rows", "cols"), None))
    return jax.shard_map(local, mesh=mesh, in_specs=in_specs, out_specs=out_specs, check_vma=False)
```

profile of v0, /device:TPU:1, one launch (start us, length us, event | category | flops | bytes accessed | tf_op | source)
XLA Modules:
  0.0 61.3 jit_solution(6253103235812254030)
XLA Ops:
  0.6 56.2 %exchange.1.z_ref = f32[64,64,256]{2,1,0:T(8,128)S(1)} custom-call(bf16[4,8,8,2048]{3,2,1,0:T(8,128)(2,1)} %bitcast.1, s32[16,64]{1,0:T(8,128)} %exps_in.1, bf16[2,2,256,256]{3,2,1,0:T(8,128)(2,1)} %constant.8.clone.send_w, bf16[2,256,256]{2,1,0:T(8,128)(2,1)} %constant.9.clone.recv_w, f32[72,128]{1,0:T(8,128)} %constant.10.clone.send_t, ...), custom_call_target="tpu_custom_call" | custom-call | tf_op jit(solution)/shard_map/exchange/pallas_call | solution.py:423
  56.9 4.4 %finish.1 = (f32[64,8192]{1,0:T(8,128)}, f32[64,8192]{1,0:T(8,128)}) custom-call(f32[64,64,256]{2,1,0:T(8,128)S(1)} %exchange.1.z_ref), custom_call_target="tpu_custom_call" | custom-call | tf_op jit(solution)/shard_map/finish/pallas_call | solution.py:490
where the time goes:
time: 61.4 us; the launch traced here: 61.3 us
  Pallas kernels  60.6 us (99%)
  between operations  0.64 us (1%)
    pallas_call x1, Pallas kernels, run_exchange(): pl.pallas_call(exchange, out_shape=jax.ShapeDtypeStruct((64, 64, 256), F3...  56.2 us
    pallas_call x1, Pallas kernels, run_finish(): pl.pallas_call(finish, grid=(8,), out_shape=[jax.ShapeDtypeStruct((64, NR...  4.4 us

commit v1 on v0

--- a/solution.py
+++ b/solution.py
@@ -250,6 +250,18 @@
             pltpu.make_async_remote_copy(
                 last.at[1], last_in.at[:, my_cols], s_last, r_last, **at((row + 1) % 32, col)
             ).start()
+
+    def wrap4(n):
+        return jnp.where(n >= 4, n - 4, n)
+
+    to_y = [wrap4(y + d) for d in range(4)]
+    corners = []
+    for flip in range(2):
+        for d in range(2):
+            to_hi = 1 - z_hi if flip else z_hi
+            to_lo = 1 - z_lo if flip else z_lo
+            to_core = 1 - core if d else core
+            corners.append((to_hi * 8 + to_core, to_hi * 4, to_lo * 2 + to_core))
 
     def send_phase(q):
         ref = block.at[:, q]
@@ -329,18 +341,25 @@
 
         lanes = pl.ds(pl.multiple_of(512 * q, 512), 512)
 
-        @pl.loop(1, 64)
-        def _(m):
-            flip, dc, dx, dy = m % 2, (m // 32) % 2, (m // 2) % 4, (m // 8) % 4
-            to_hi, to_lo, to_core = (z_hi + flip) % 2, (z_lo + flip) % 2, (core + dc) % 2
-            to_row = (x + dx) % 4 * 8 + to_hi * 4 + (y + dy) % 4
-            pltpu.make_async_remote_copy(
-                outbox.at[:, pl.ds(to_row * 2 + to_core, 1), lanes],
-                inbox.at[:, pl.ds(me, 1), lanes],
-                s_out.at[q],
-                r_out.at[q],
-                **at(to_row, to_lo * 2 + to_core),
-            ).start()
+        @pl.loop(0, 4)
+        def _(k):
+            for dy in range(4):
+                place = wrap4(x + wrap4(k + dy)) * 8 + to_y[dy]
+                for n, (add_t, add_row, to_col) in enumerate(corners):
+
+                    def go(place=place, add_t=add_t, add_row=add_row, to_col=to_col):
+                        pltpu.make_async_remote_copy(
+                            outbox.at[:, pl.ds(place * 2 + add_t, 1), lanes],
+                            inbox.at[:, pl.ds(me, 1), lanes],
+                            s_out.at[q],
+                            r_out.at[q],
+                            **at(place + add_row, to_col),
+                        ).start()
+
+                    if dy == 0 and n == 0:
+                        pl.when(k != 0)(go)
+                    else:
+                        go()
 
         pltpu.make_async_copy(
             outbox.at[:, pl.ds(me, 1), lanes], inbox.at[:, pl.ds(me, 1), lanes], r_out.at[q]

time: 61.4 us -> 49.8 us (0.81)
  Pallas kernels: 60.6 us -> 49.1 us
    pallas_call x1, Pallas kernels: 56.2 us -> 44.7 us  [run_exchange(): pl.pallas_call(exchange, out_shape=jax.ShapeDtypeStruct((64, 64, 256), F3...]
where the time goes in v1:
time: 49.8 us; the launch traced here: 49.7 us
  Pallas kernels  49.1 us (99%)
  between operations  0.64 us (1%)
    pallas_call x1, Pallas kernels, run_exchange(): pl.pallas_call(exchange, out_shape=jax.ShapeDtypeStruct((64, 64, 256), F3...  44.7 us
    pallas_call x1, Pallas kernels, run_finish(): pl.pallas_call(finish, grid=(8,), out_shape=[jax.ShapeDtypeStruct((64, NR...  4.4 us

profile of v1, /device:TPU:1, one launch (start us, length us, event | category | flops | bytes accessed | tf_op | source)
XLA Modules:
  0.0 49.7 jit_solution(1726928185158147027)
XLA Ops:
  0.6 44.7 %exchange.1.z_ref = f32[64,64,256]{2,1,0:T(8,128)S(1)} custom-call(bf16[4,8,8,2048]{3,2,1,0:T(8,128)(2,1)} %bitcast.1, s32[16,64]{1,0:T(8,128)} %exps_in.1, bf16[2,2,256,256]{3,2,1,0:T(8,128)(2,1)} %constant.8.clone.send_w, bf16[2,256,256]{2,1,0:T(8,128)(2,1)} %constant.9.clone.recv_w, f32[72,128]{1,0:T(8,128)} %constant.10.clone.send_t, ...), custom_call_target="tpu_custom_call" | custom-call | tf_op jit(solution)/shard_map/exchange/pallas_call | solution.py:442
  45.3 4.4 %finish.1 = (f32[64,8192]{1,0:T(8,128)}, f32[64,8192]{1,0:T(8,128)}) custom-call(f32[64,64,256]{2,1,0:T(8,128)S(1)} %exchange.1.z_ref), custom_call_target="tpu_custom_call" | custom-call | tf_op jit(solution)/shard_map/finish/pallas_call | solution.py:509

commit v2 on v0

--- a/solution.py
+++ b/solution.py
@@ -13,9 +13,10 @@
 NC = 8192
 MESH = pl.DeviceIdType.MESH
 CHUNKS = 8
-LAG = 2
+LAG = 4
 TOP = 32767.0
 BOUND = 16896.0
+DECODED = BOUND / TOP**4
 F32 = jnp.float32
 BF16 = jnp.bfloat16
 
@@ -23,7 +24,7 @@
 def halves(table):
     high = table.astype(ml_dtypes.bfloat16)
     low = (table - high.astype(np.float64)).astype(ml_dtypes.bfloat16)
-    return np.stack([high, low])
+    return np.concatenate([high, high, low], 0)
 
 
 def send_table():
@@ -38,7 +39,7 @@
         two = 2 * np.pi * (jo * (a + 1) % 128) / 128
         from_re = np.concatenate([np.cos(one), -np.sin(one), np.cos(two), -np.sin(two)], 1)
         from_im = np.concatenate([np.sin(one), np.cos(one), -np.sin(two), -np.cos(two)], 1)
-        sides.append(halves(np.concatenate([from_re, from_im], 0)))
+        sides.append(halves(np.concatenate([from_re, from_im], 0) / DECODED))
     return np.stack(sides)
 
 
@@ -114,17 +115,14 @@
 
 
 def code(x):
-    u = lax.rsqrt(lax.rsqrt(jnp.maximum(jnp.abs(x) * (1.0 / BOUND), 1e-30)))
-    n = (u * TOP + 0.5).astype(jnp.int32)
+    u = lax.rsqrt(lax.rsqrt(jnp.maximum(jnp.abs(x), 1e-12)))
+    n = (u + 0.5).astype(jnp.int32)
     return jnp.where(x < 0, -n, n)
 
 
 def decode(n):
     v = n.astype(F32)
     return (v * jnp.abs(v)) * (v * v)
-
-
-DECODED = BOUND / TOP**4
 
 
 def split(x):
@@ -136,8 +134,8 @@
     mant, exps_in, send_w, recv_w, send_t, recv_t,
     z_out,
     block, masses, first, a_hi, a_lo, products, words, outbox, inbox, b_hi, b_lo, result,
-    exps, w_ref, e_ref, t1_ref, t2_ref, edge_in, edge, above, last, last_in,
-    s_blk, r_blk, s_out, r_out, s_edge, r_edge, s_last, r_last, tab_sem, edge_sem, z_sem, exp_sem, sem_b, sem_c, sem_d,
+    exps, scale_v, scales, w_ref, e_ref, t1_ref, t2_ref, edge_in, edge, above, last, last_in,
+    s_blk, r_blk, s_out, r_out, s_edge, r_edge, s_last, r_last, tab_sem, edge_sem, z_sem, exp_sem, sem_b, sem_s, sem_c, sem_d,
 ):
     row, col = lax.axis_index("rows"), lax.axis_index("cols")
     x, z_hi, y = row // 8, (row // 4) % 2, row % 4
@@ -148,6 +146,9 @@
 
     def at(r, c):
         return dict(device_id={"rows": r, "cols": c}, device_id_type=MESH)
+
+    def wrap4(n):
+        return jnp.where(n >= 4, n - 4, n)
 
     def mate(m):
         other = (core + m % 2) % 2
@@ -163,49 +164,49 @@
         pltpu.make_async_copy(mant.at[:, 0], edge_in.at[0], edge_sem.at[0]),
         pltpu.make_async_copy(mant.at[:, 7], edge_in.at[1], edge_sem.at[1]),
     )
-    exp_copy = pltpu.make_async_copy(exps_in, exps, exp_sem)
+    exp_copy = pltpu.make_async_copy(exps_in, exps, exp_sem.at[0])
     exp_copy.start()
     for copy in edges + tables:
         copy.start()
 
     barrier = pltpu.get_barrier_semaphore()
-    count = 0
-    for m in (1, 2, 3):
-        pl.semaphore_signal(barrier, inc=1, **at(row, mate(m)[0]))
-        count += 1
-    for other in (core, 1 - core):
-        pl.semaphore_signal(barrier, inc=1, **at(x * 8 + (1 - z_hi) * 4 + y, (1 - z_lo) * 2 + other))
-        count += 1
-    for d in (1, 2, 3):
-        pl.semaphore_signal(barrier, inc=1, **at(x * 8 + z_hi * 4 + (y + d) % 4, col))
-        pl.semaphore_signal(barrier, inc=1, **at((x + d) % 4 * 8 + z_hi * 4 + y, col))
-        count += 2
+    away = at(x * 8 + (1 - z_hi) * 4 + y, (1 - z_lo) * 2 + core)
+    sibling = at(row, z_lo * 2 + 1 - core)
+    to_y = [wrap4(y + d) for d in range(4)]
+    to_x = [wrap4(x + d) for d in range(4)]
+    ring_x = [at(to_x[d] * 8 + z_hi * 4 + y, col) for d in (2, 1, 3)]
+    ring_y = [at(x * 8 + z_hi * 4 + to_y[d], col) for d in (2, 1, 3)]
+    group = [at(row, (1 - z_lo) * 2 + core), at(row, (1 - z_lo) * 2 + 1 - core), sibling]
+    first_round = [away] + ring_x + ring_y + group
+    for target in first_round:
+        pl.semaphore_signal(barrier, inc=1, **target)
 
     exp_copy.wait()
+    scale_v[...] = jnp.left_shift(1, exps[...] + 3).astype(F32) * 0.125
+    scale_copy = pltpu.make_async_copy(scale_v, scales, exp_sem.at[1])
+    scale_copy.start()
+    scale_copy.wait()
     for copy in edges:
         copy.wait()
     for g in range(4):
         for j in range(16):
             lanes = slice(128 * j, 128 * (j + 1))
-            e = exps[4 * g, 16 * col + j]
-            scale = jnp.left_shift(1, e + 3).astype(F32) * 0.125
-            edge[g // 2, g % 2 : g % 2 + 1, lanes] = edge_in[0, g, :, lanes].astype(F32)[7:8] * scale
+            scale = scales[4 * g, 16 * col + j]
+            edge[g // 2, g % 2, :, lanes] = edge_in[0, g, :, lanes].astype(F32)[7:8] * scale
             if g % 2:
-                e = exps[4 * g + 3, 16 * col + j]
-                scale = jnp.left_shift(1, e + 3).astype(F32) * 0.125
+                scale = scales[4 * g + 3, 16 * col + j]
                 last[g // 2, :, lanes] = edge_in[1, g, :, lanes].astype(F32)[7:8] * scale
 
-    pl.semaphore_wait(barrier, count)
+    pl.semaphore_wait(barrier, len(first_round))
     for m in (1, 2, 3):
         c, other = mate(m)
         pltpu.make_async_remote_copy(
-            edge.at[other], above.at[:, my_cols], s_edge, r_edge, **at(row, c)
+            edge.at[other], above.at[:, pl.ds(7, 1), my_cols], s_edge, r_edge, **at(row, c)
         ).start()
-    pltpu.make_async_copy(edge.at[core], above.at[:, my_cols], r_edge).start()
+    pltpu.make_async_copy(edge.at[core], above.at[:, pl.ds(7, 1), my_cols], r_edge).start()
 
     def send_block(q):
-        for m in (2, 3, 1):
-            c, other = mate(m)
+        for c, other in (((1 - z_lo) * 2, 0), ((1 - z_lo) * 2 + 1, 1), (z_lo * 2 + 1 - core, 1 - core)):
             pltpu.make_async_remote_copy(
                 mant.at[pl.ds(2 * other, 2), q], block.at[:, q, :, my_cols], s_blk.at[q], r_blk.at[q], **at(row, c)
             ).start()
@@ -213,25 +214,25 @@
             mant.at[pl.ds(2 * core, 2), q], block.at[:, q, :, my_cols], r_blk.at[q]
         ).start()
 
-    @pl.loop(0, CHUNKS)
+    send_block(1)
+    for target in ring_y:
+        pl.semaphore_signal(sem_b, inc=1, **target)
+
+    @pl.loop(1, CHUNKS)
     def _(j):
         send_block((j + 1) % CHUNKS)
 
-    for d in (1, 2, 3):
-        pl.semaphore_signal(sem_b, inc=1, **at(x * 8 + z_hi * 4 + (y + d) % 4, col))
     pl.semaphore_wait(sem_b, 3)
-    for d in (1, 2, 3):
-        pl.semaphore_signal(sem_c, inc=1, **at((x + d) % 4 * 8 + z_hi * 4 + y, col))
+    pl.semaphore_signal(sem_s, inc=1, **sibling)
+    pl.semaphore_wait(sem_s, 1)
+    pl.semaphore_signal(sem_c, inc=1, **away)
 
     for copy in tables:
         copy.wait()
-    ref = above
+    ref = above.at[:, pl.ds(7, 1)]
     pltpu.make_async_copy(ref, ref, r_edge).wait()
     sub8 = lax.broadcasted_iota(jnp.int32, (8, 128), 0)
     lane8 = lax.broadcasted_iota(jnp.int32, (8, 128), 1)
-
-    pl.semaphore_wait(sem_c, 3)
-    pl.semaphore_signal(sem_d, inc=1, **at(x * 8 + (1 - z_hi) * 4 + y, (1 - z_lo) * 2 + core))
 
     def send_last():
         pl.semaphore_wait(sem_d, 1)
@@ -251,7 +252,15 @@
                 last.at[1], last_in.at[:, my_cols], s_last, r_last, **at((row + 1) % 32, col)
             ).start()
 
-    def send_phase(q):
+    corners = []
+    for flip in range(2):
+        for d in range(2):
+            to_hi = 1 - z_hi if flip else z_hi
+            to_lo = 1 - z_lo if flip else z_lo
+            to_core = 1 - core if d else core
+            corners.append((to_hi * 64 + to_core * 8, to_hi * 4, to_lo * 2 + to_core))
+
+    def send_phase(q, j):
         ref = block.at[:, q]
         pltpu.make_async_copy(ref, ref, r_blk.at[q]).wait()
 
@@ -259,12 +268,11 @@
             before = None
             for c in range(64):
                 lanes = slice(128 * c, 128 * (c + 1))
-                e = exps[8 * core + 4 * h + q // 2, c]
-                scale = jnp.left_shift(1, e + 3).astype(F32) * 0.125
+                scale = scales[8 * core + 4 * h + q // 2, c]
                 here = block[h, q, :, lanes].astype(F32) * scale
-                top = jnp.broadcast_to(above[h : h + 1, lanes], (8, 128))
+                top = jnp.broadcast_to(above[h, 7:8, lanes], (8, 128))
                 upper = jnp.where(sub8 == 0, top, pltpu.roll(here, 1, 0))
-                above[h : h + 1, lanes] = here[7:8]
+                above[h, :, lanes] = here
                 step = here - upper
                 rolled = pltpu.roll(step, 1, 1)
                 left = jnp.where(lane8 == 0, 0.0 if before is None else before, rolled)
@@ -307,11 +315,8 @@
                 a_hi[rows, 128:256], a_lo[rows, 128:256] = split(tw_im)
 
         high = a_hi[...]
-        products[...] = (
-            jnp.dot(high, w_ref[0], preferred_element_type=F32)
-            + jnp.dot(a_lo[...], w_ref[0], preferred_element_type=F32)
-            + jnp.dot(high, w_ref[1], preferred_element_type=F32)
-        )
+        parts = jnp.concatenate([high, a_lo[...], high], 1)
+        products[...] = jnp.dot(parts, w_ref[...], preferred_element_type=F32)
 
         for b in range(33):
             for place, lanes in ((b, slice(0, 128)), (64 - b, slice(128, 256))):
@@ -320,50 +325,64 @@
                 low = code(products[16 * b : 16 * b + 8, lanes])
                 top = code(products[16 * b + 8 : 16 * b + 16, lanes])
                 words[8 * place : 8 * place + 8, :] = jnp.left_shift(top, 16) | (low & 0xFFFF)
+        start = pl.multiple_of(512 * q, 512)
         for p in range(4):
             tile = jnp.concatenate(
                 [words[pl.ds(64 * g + i, 8, stride=8), :] for i in (2 * p, 2 * p + 1) for g in range(8)], 0
             )
-            lanes = pl.ds(pl.multiple_of(512 * q + 128 * p, 128), 128)
-            outbox[:, :, lanes] = tile.T.reshape(2, 64, 128)
-
-        lanes = pl.ds(pl.multiple_of(512 * q, 512), 512)
-
-        @pl.loop(1, 64)
-        def _(m):
-            flip, dc, dx, dy = m % 2, (m // 32) % 2, (m // 2) % 4, (m // 8) % 4
-            to_hi, to_lo, to_core = (z_hi + flip) % 2, (z_lo + flip) % 2, (core + dc) % 2
-            to_row = (x + dx) % 4 * 8 + to_hi * 4 + (y + dy) % 4
-            pltpu.make_async_remote_copy(
-                outbox.at[:, pl.ds(to_row * 2 + to_core, 1), lanes],
-                inbox.at[:, pl.ds(me, 1), lanes],
-                s_out.at[q],
-                r_out.at[q],
-                **at(to_row, to_lo * 2 + to_core),
-            ).start()
-
-        pltpu.make_async_copy(
-            outbox.at[:, pl.ds(me, 1), lanes], inbox.at[:, pl.ds(me, 1), lanes], r_out.at[q]
-        ).start()
+            tile = tile.T
+            for n in range(16):
+                outbox[pl.ds(start + 64 * (n % 8) + 4 * (n // 8) + p, 8, stride=8), :] = tile[8 * n : 8 * n + 8]
+
+        mine = pl.ds(pl.multiple_of(512 * q + 8 * me, 8), 8)
+
+        for flip in range(2):
+            if flip:
+
+                @pl.when(j == 0)
+                def _():
+                    pl.semaphore_wait(sem_c, 1)
+                    pl.semaphore_signal(sem_d, inc=1, **group[0])
+
+            @pl.loop(0, 4)
+            def _(k, flip=flip):
+                for dy in range(4):
+                    place = wrap4(x + wrap4(k + dy)) * 8 + to_y[dy]
+                    for n, (add_t, add_row, to_col) in enumerate(corners[2 * flip : 2 * flip + 2]):
+                        add_t = add_t + 512 * q
+
+                        def go(place=place, add_t=add_t, add_row=add_row, to_col=to_col):
+                            pltpu.make_async_remote_copy(
+                                outbox.at[pl.ds(pl.multiple_of(place * 16 + add_t, 8), 8)],
+                                inbox.at[mine],
+                                s_out.at[q],
+                                r_out.at[q],
+                                **at(place + add_row, to_col),
+                            ).start()
+
+                        if flip == 0 and dy == 0 and n == 0:
+                            pl.when(k != 0)(go)
+                        else:
+                            go()
+
+        pltpu.make_async_copy(outbox.at[mine], inbox.at[mine], r_out.at[q]).start()
 
     def receive_phase(q):
-        lanes = pl.ds(pl.multiple_of(512 * q, 512), 512)
-        ref = inbox.at[:, :, lanes]
+        start = pl.multiple_of(512 * q, 512)
+        ref = inbox.at[pl.ds(start, 512)]
         pltpu.make_async_copy(ref, ref, r_out.at[q]).wait()
         for p in range(4):
-            lanes = pl.ds(pl.multiple_of(512 * q + 128 * p, 128), 128)
-            tile = inbox[:, :, lanes].reshape(128, 128).T
+            tile = jnp.concatenate(
+                [inbox[pl.ds(start + 64 * (n % 8) + 4 * (n // 8) + p, 8, stride=8), :] for n in range(16)], 0
+            ).T
             rows = slice(128 * p, 128 * p + 128)
             low = decode(jnp.right_shift(jnp.left_shift(tile, 16), 16))
             b_hi[rows, 0:128], b_lo[rows, 0:128] = split(low)
             top = decode(jnp.right_shift(tile, 16))
             b_hi[rows, 128:256], b_lo[rows, 128:256] = split(top)
         high = b_hi[...]
-        value = (
-            jnp.dot(high, e_ref[0], preferred_element_type=F32)
-            + jnp.dot(b_lo[...], e_ref[0], preferred_element_type=F32)
-            + jnp.dot(high, e_ref[1], preferred_element_type=F32)
-        )
+        parts = jnp.concatenate([high, b_lo[...], high], 1)
+        value = jnp.dot(parts, e_ref[...], preferred_element_type=F32)
         for i in range(8):
             re, im = value[64 * i : 64 * i + 64, 0:128], value[64 * i : 64 * i + 64, 128:256]
             cos = t2_ref[pl.ds(16 * q + 2 * i, 1), :]
@@ -378,8 +397,8 @@
         @pl.when(j == CHUNKS - 1)
         def _():
             pltpu.make_async_copy(last_in, last_in, r_last).wait()
-            above[1:2, :] = above[0:1, :]
-            above[0:1, :] = jnp.where(row * 2 + core == 0, jnp.zeros_like(last_in[...]), last_in[...])
+            above[1, 7:8, :] = above[0, 7:8, :]
+            above[0, 7:8, :] = jnp.where(row * 2 + core == 0, jnp.zeros_like(last_in[...]), last_in[...])
 
         @pl.when(j == 2)
         def _():
@@ -387,7 +406,7 @@
 
         @pl.when(j < CHUNKS)
         def _():
-            send_phase((j + 1) % CHUNKS)
+            send_phase((j + 1) % CHUNKS, j)
 
         @pl.when(j >= LAG)
         def _():
@@ -398,7 +417,7 @@
     for q in range(CHUNKS):
         ref = block.at[:, q, :, pl.ds(0, 6144)]
         pltpu.make_async_copy(ref, ref, s_blk.at[q]).wait()
-        ref = outbox.at[0, pl.ds(0, 24), pl.ds(0, 2688)]
+        ref = outbox.at[pl.ds(0, 504)]
         pltpu.make_async_copy(ref, ref, s_out.at[q]).wait()
         ref = pl.ds(8 * q, 8)
         pltpu.make_async_copy(result.at[ref], z_out.at[ref], z_sem.at[q]).wait()
@@ -433,19 +452,21 @@
             pltpu.VMEM((528, 256), BF16),
             pltpu.VMEM((528, 256), F32),
             pltpu.VMEM((512, 128), jnp.int32),
-            pltpu.VMEM((2, 64, 4096), jnp.int32),
-            pltpu.VMEM((2, 64, 4096), jnp.int32),
+            pltpu.VMEM((4096, 128), jnp.int32),
+            pltpu.VMEM((4096, 128), jnp.int32),
             pltpu.VMEM((512, 256), BF16),
             pltpu.VMEM((512, 256), BF16),
             pltpu.VMEM((64, 64, 256), F32),
-            pltpu.SMEM((16, 64), jnp.int32),
-            pltpu.VMEM((2, 256, 256), BF16),
-            pltpu.VMEM((2, 256, 256), BF16),
+            pltpu.VMEM((16, 64), jnp.int32),
+            pltpu.VMEM((16, 64), F32),
+            pltpu.SMEM((16, 64), F32),
+            pltpu.VMEM((768, 256), BF16),
+            pltpu.VMEM((768, 256), BF16),
             pltpu.VMEM((72, 128), F32),
             pltpu.VMEM((128, 128), F32),
             pltpu.VMEM((2, 4, 8, 2048), BF16),
-            pltpu.VMEM((2, 2, 2048), F32),
-            pltpu.VMEM((2, 8192), F32),
+            pltpu.VMEM((2, 2, 1, 2048), F32),
+            pltpu.VMEM((2, 8, 8192), F32),
             pltpu.VMEM((2, 1, 2048), F32),
             pltpu.VMEM((1, 8192), F32),
             dma((CHUNKS,)),
@@ -459,7 +480,8 @@
             dma((4,)),
             dma((2,)),
             dma((CHUNKS,)),
-            dma,
+            dma((2,)),
+            pltpu.SemaphoreType.REGULAR,
             pltpu.SemaphoreType.REGULAR,
             pltpu.SemaphoreType.REGULAR,
             pltpu.SemaphoreType.REGULAR,
@@ -471,29 +493,51 @@
     )(*[pltpu.with_memory_space_constraint(operand, pltpu.HBM) for operand in operands])
 
 
-def finish(z_ref, re_ref, im_ref, middle):
-    for i0 in range(8):
-        spread = dft8([(z_ref[8 * i1 + i0, :, 0:128], z_ref[8 * i1 + i0, :, 128:256]) for i1 in range(8)])
+def finish(z_ref, re_out, im_out, re_ref, im_ref, middle, sems):
+    def leave(g):
+        rows = pl.ds(8 * g, 8)
+        return (
+            pltpu.make_async_copy(re_ref.at[rows], re_out.at[rows], sems.at[0, g]),
+            pltpu.make_async_copy(im_ref.at[rows], im_out.at[rows], sems.at[1, g]),
+        )
+
+    @pl.loop(0, 8)
+    def _(g):
+        rows = pl.ds(pl.multiple_of(8 * g, 8), 8)
+        for i0 in range(8):
+            spread = dft8(
+                [(z_ref[8 * i1 + i0, rows, 0:128], z_ref[8 * i1 + i0, rows, 128:256]) for i1 in range(8)]
+            )
+            for k_a in range(8):
+                value = twist64(spread[k_a], i0 * k_a)
+                middle[k_a, i0, 0] = value[0]
+                middle[k_a, i0, 1] = value[1]
         for k_a in range(8):
-            value = twist64(spread[k_a], i0 * k_a)
-            middle[k_a, i0, 0] = value[0]
-            middle[k_a, i0, 1] = value[1]
-    for k_a in range(8):
-        spread = dft8([(middle[k_a, i0, 0], middle[k_a, i0, 1]) for i0 in range(8)])
-        for k_b, (re, im) in enumerate(spread):
-            lanes = slice(128 * (k_a + 8 * k_b), 128 * (k_a + 8 * k_b + 1))
-            re_ref[:, lanes] = re
-            im_ref[:, lanes] = im
+            spread = dft8([(middle[k_a, i0, 0], middle[k_a, i0, 1]) for i0 in range(8)])
+            for k_b, (re, im) in enumerate(spread):
+                lanes = slice(128 * (k_a + 8 * k_b), 128 * (k_a + 8 * k_b + 1))
+                re_ref[rows, lanes] = re
+                im_ref[rows, lanes] = im
+        for copy in leave(g):
+            copy.start()
+
+    for g in range(8):
+        for copy in leave(g):
+            copy.wait()
 
 
 def run_finish(z):
     return pl.pallas_call(
         finish,
-        grid=(8,),
         out_shape=[jax.ShapeDtypeStruct((64, NR), F32)] * 2,
-        in_specs=[pl.BlockSpec((64, 8, 256), lambda g: (0, g, 0))],
-        out_specs=[pl.BlockSpec((8, NR), lambda g: (g, 0))] * 2,
-        scratch_shapes=[pltpu.VMEM((8, 8, 2, 8, 128), F32)],
+        in_specs=[pl.BlockSpec(memory_space=pltpu.VMEM)],
+        out_specs=[pl.BlockSpec(memory_space=pl.ANY)] * 2,
+        scratch_shapes=[
+            pltpu.VMEM((64, NR), F32),
+            pltpu.VMEM((64, NR), F32),
+            pltpu.VMEM((8, 8, 2, 8, 128), F32),
+            pltpu.SemaphoreType.DMA((2, 8)),
+        ],
         compiler_params=pltpu.CompilerParams(vmem_limit_bytes=48 * 1024 * 1024),
         name="finish",
     )(z)

time: 61.4 us -> 45.3 us (0.74)
  Pallas kernels: 60.6 us -> 44.5 us
    pallas_call x1, Pallas kernels: 56.2 us -> 42 us  [run_exchange(): pl.pallas_call(exchange, out_shape=jax.ShapeDtypeStruct((64, 64, 256), F3...]
    pallas_call x1, Pallas kernels: 4.4 us -> 2.55 us  [run_finish(): pl.pallas_call(finish, out_shape=[jax.ShapeDtypeStruct((64, NR), F32)] *...]
where the time goes in v2:
time: 45.3 us; the launch traced here: 45.2 us
  Pallas kernels  44.5 us (98%)
  between operations  0.64 us (1%)
    pallas_call x1, Pallas kernels, run_exchange(): pl.pallas_call(exchange, out_shape=jax.ShapeDtypeStruct((64, 64, 256), F3...  42 us
    pallas_call x1, Pallas kernels, run_finish(): pl.pallas_call(finish, out_shape=[jax.ShapeDtypeStruct((64, NR), F32)] *...  2.55 us

profile of v2, /device:TPU:1, one launch (start us, length us, event | category | flops | bytes accessed | tf_op | source)
XLA Modules:
  0.0 45.2 jit_solution(10683047297015889229)
XLA Ops:
  0.6 42.0 %exchange.1.z_ref = f32[64,64,256]{2,1,0:T(8,128)S(1)} custom-call(bf16[4,8,8,2048]{3,2,1,0:T(8,128)(2,1)} %bitcast.1, s32[16,64]{1,0:T(8,128)} %exps_in.1, bf16[2,768,256]{2,1,0:T(8,128)(2,1)} %constant.8.clone.send_w, bf16[768,256]{1,0:T(8,128)(2,1)} %constant.9.clone.recv_w, f32[72,128]{1,0:T(8,128)} %constant.10.clone.send_t, ...), custom_call_target="tpu_custom_call" | custom-call | tf_op jit(solution)/shard_map/exchange/pallas_call | solution.py:442
  42.6 2.6 %finish.1 = (f32[64,8192]{1,0:T(8,128)}, f32[64,8192]{1,0:T(8,128)}) custom-call(f32[64,64,256]{2,1,0:T(8,128)S(1)} %exchange.1.z_ref), custom_call_target="tpu_custom_call" | custom-call | tf_op jit(solution)/shard_map/finish/pallas_call | solution.py:530

commit v3 on v2

--- a/solution.py
+++ b/solution.py
@@ -133,9 +133,9 @@
 def exchange(
     mant, exps_in, send_w, recv_w, send_t, recv_t,
     z_out,
-    block, masses, first, a_hi, a_lo, products, words, outbox, inbox, b_hi, b_lo, result,
-    exps, scale_v, scales, w_ref, e_ref, t1_ref, t2_ref, edge_in, edge, above, last, last_in,
-    s_blk, r_blk, s_out, r_out, s_edge, r_edge, s_last, r_last, tab_sem, edge_sem, z_sem, exp_sem, sem_b, sem_s, sem_c, sem_d,
+    block, masses, first, a_hi, a_lo, products, words, outbox, inbox, b_hi, b_lo,
+    exps, scale_v, scales, w_ref, e_ref, t1_ref, t2_ref, edge_in, edge, edge_got, above, last, last_in,
+    s_blk, r_blk, s_out, r_out, s_edge, r_edge, s_last, r_last, tab_sem, edge_sem, exp_sem, sem_b, sem_s, sem_c, sem_d,
 ):
     row, col = lax.axis_index("rows"), lax.axis_index("cols")
     x, z_hi, y = row // 8, (row // 4) % 2, row % 4
@@ -153,6 +153,18 @@
     def mate(m):
         other = (core + m % 2) % 2
         return ((z_lo + m // 2) % 2) * 2 + other, other
+
+    barrier = pltpu.get_barrier_semaphore()
+    away = at(x * 8 + (1 - z_hi) * 4 + y, (1 - z_lo) * 2 + core)
+    sibling = at(row, z_lo * 2 + 1 - core)
+    to_y = [wrap4(y + d) for d in range(4)]
+    to_x = [wrap4(x + d) for d in range(4)]
+    ring_x = [at(to_x[d] * 8 + z_hi * 4 + y, col) for d in (2, 1, 3)]
+    ring_y = [at(x * 8 + z_hi * 4 + to_y[d], col) for d in (2, 1, 3)]
+    group = [at(row, (1 - z_lo) * 2 + core), at(row, (1 - z_lo) * 2 + 1 - core), sibling]
+    first_round = [away] + ring_x + ring_y + group
+    for target in first_round:
+        pl.semaphore_signal(barrier, inc=1, **target)
 
     tables = (
         pltpu.make_async_copy(send_w.at[side], w_ref, tab_sem.at[0]),
@@ -169,18 +181,6 @@
     for copy in edges + tables:
         copy.start()
 
-    barrier = pltpu.get_barrier_semaphore()
-    away = at(x * 8 + (1 - z_hi) * 4 + y, (1 - z_lo) * 2 + core)
-    sibling = at(row, z_lo * 2 + 1 - core)
-    to_y = [wrap4(y + d) for d in range(4)]
-    to_x = [wrap4(x + d) for d in range(4)]
-    ring_x = [at(to_x[d] * 8 + z_hi * 4 + y, col) for d in (2, 1, 3)]
-    ring_y = [at(x * 8 + z_hi * 4 + to_y[d], col) for d in (2, 1, 3)]
-    group = [at(row, (1 - z_lo) * 2 + core), at(row, (1 - z_lo) * 2 + 1 - core), sibling]
-    first_round = [away] + ring_x + ring_y + group
-    for target in first_round:
-        pl.semaphore_signal(barrier, inc=1, **target)
-
     exp_copy.wait()
     scale_v[...] = jnp.left_shift(1, exps[...] + 3).astype(F32) * 0.125
     scale_copy = pltpu.make_async_copy(scale_v, scales, exp_sem.at[1])
@@ -192,7 +192,7 @@
         for j in range(16):
             lanes = slice(128 * j, 128 * (j + 1))
             scale = scales[4 * g, 16 * col + j]
-            edge[g // 2, g % 2, :, lanes] = edge_in[0, g, :, lanes].astype(F32)[7:8] * scale
+            edge[g // 2, g % 2, :, lanes] = (edge_in[0, g, :, lanes].astype(F32)[7:8] * scale).astype(BF16)
             if g % 2:
                 scale = scales[4 * g + 3, 16 * col + j]
                 last[g // 2, :, lanes] = edge_in[1, g, :, lanes].astype(F32)[7:8] * scale
@@ -201,9 +201,9 @@
     for m in (1, 2, 3):
         c, other = mate(m)
         pltpu.make_async_remote_copy(
-            edge.at[other], above.at[:, pl.ds(7, 1), my_cols], s_edge, r_edge, **at(row, c)
+            edge.at[other], edge_got.at[:, :, my_cols], s_edge, r_edge, **at(row, c)
         ).start()
-    pltpu.make_async_copy(edge.at[core], above.at[:, pl.ds(7, 1), my_cols], r_edge).start()
+    pltpu.make_async_copy(edge.at[core], edge_got.at[:, :, my_cols], r_edge).start()
 
     def send_block(q):
         for c, other in (((1 - z_lo) * 2, 0), ((1 - z_lo) * 2 + 1, 1), (z_lo * 2 + 1 - core, 1 - core)):
@@ -229,8 +229,9 @@
 
     for copy in tables:
         copy.wait()
-    ref = above.at[:, pl.ds(7, 1)]
-    pltpu.make_async_copy(ref, ref, r_edge).wait()
+    pltpu.make_async_copy(edge_got, edge_got, r_edge).wait()
+    for h in range(2):
+        above[h, 7:8, :] = edge_got[h].astype(F32)
     sub8 = lax.broadcasted_iota(jnp.int32, (8, 128), 0)
     lane8 = lax.broadcasted_iota(jnp.int32, (8, 128), 1)
 
@@ -252,13 +253,8 @@
                 last.at[1], last_in.at[:, my_cols], s_last, r_last, **at((row + 1) % 32, col)
             ).start()
 
-    corners = []
-    for flip in range(2):
-        for d in range(2):
-            to_hi = 1 - z_hi if flip else z_hi
-            to_lo = 1 - z_lo if flip else z_lo
-            to_core = 1 - core if d else core
-            corners.append((to_hi * 64 + to_core * 8, to_hi * 4, to_lo * 2 + to_core))
+    hops = (0, 1, 2, 1)
+    plane = sorted(((dx, dy) for dx in range(4) for dy in range(4)), key=lambda o: -hops[o[0]] - hops[o[1]])
 
     def send_phase(q, j):
         ref = block.at[:, q]
@@ -336,34 +332,35 @@
 
         mine = pl.ds(pl.multiple_of(512 * q + 8 * me, 8), 8)
 
-        for flip in range(2):
-            if flip:
-
-                @pl.when(j == 0)
-                def _():
-                    pl.semaphore_wait(sem_c, 1)
-                    pl.semaphore_signal(sem_d, inc=1, **group[0])
-
-            @pl.loop(0, 4)
-            def _(k, flip=flip):
-                for dy in range(4):
-                    place = wrap4(x + wrap4(k + dy)) * 8 + to_y[dy]
-                    for n, (add_t, add_row, to_col) in enumerate(corners[2 * flip : 2 * flip + 2]):
-                        add_t = add_t + 512 * q
-
-                        def go(place=place, add_t=add_t, add_row=add_row, to_col=to_col):
-                            pltpu.make_async_remote_copy(
-                                outbox.at[pl.ds(pl.multiple_of(place * 16 + add_t, 8), 8)],
-                                inbox.at[mine],
-                                s_out.at[q],
-                                r_out.at[q],
-                                **at(place + add_row, to_col),
-                            ).start()
-
-                        if flip == 0 and dy == 0 and n == 0:
-                            pl.when(k != 0)(go)
-                        else:
-                            go()
+        @pl.loop(0, 2)
+        def _(turn):
+            flip = turn
+
+            @pl.when((j == 0) & (turn == 1))
+            def _():
+                pl.semaphore_wait(sem_c, 1)
+                pl.semaphore_signal(sem_d, inc=1, **group[0])
+
+            to_hi = jnp.where(flip == 1, 1 - z_hi, z_hi)
+            to_lo = jnp.where(flip == 1, 1 - z_lo, z_lo)
+            for dx, dy in plane:
+                place = to_x[dx] * 8 + to_y[dy] + to_hi * 4
+                for d in range(2):
+                    to_core = 1 - core if d else core
+
+                    def go(place=place, to_core=to_core):
+                        pltpu.make_async_remote_copy(
+                            outbox.at[pl.ds(pl.multiple_of(512 * q + place * 16 + to_core * 8, 8), 8)],
+                            inbox.at[mine],
+                            s_out.at[q],
+                            r_out.at[q],
+                            **at(place, to_lo * 2 + to_core),
+                        ).start()
+
+                    if (dx, dy, d) == (0, 0, 0):
+                        pl.when(flip == 1)(go)
+                    else:
+                        go()
 
         pltpu.make_async_copy(outbox.at[mine], inbox.at[mine], r_out.at[q]).start()
 
@@ -387,10 +384,8 @@
             re, im = value[64 * i : 64 * i + 64, 0:128], value[64 * i : 64 * i + 64, 128:256]
             cos = t2_ref[pl.ds(16 * q + 2 * i, 1), :]
             sin = t2_ref[pl.ds(16 * q + 2 * i + 1, 1), :]
-            result[8 * q + i, :, 0:128] = re * cos - im * sin
-            result[8 * q + i, :, 128:256] = re * sin + im * cos
-        ref = pl.ds(8 * q, 8)
-        pltpu.make_async_copy(result.at[ref], z_out.at[ref], z_sem.at[q]).start()
+            z_out[8 * q + i, :, 0:128] = re * cos - im * sin
+            z_out[8 * q + i, :, 128:256] = re * sin + im * cos
 
     @pl.loop(0, CHUNKS + LAG)
     def _(j):
@@ -419,8 +414,6 @@
         pltpu.make_async_copy(ref, ref, s_blk.at[q]).wait()
         ref = outbox.at[pl.ds(0, 504)]
         pltpu.make_async_copy(ref, ref, s_out.at[q]).wait()
-        ref = pl.ds(8 * q, 8)
-        pltpu.make_async_copy(result.at[ref], z_out.at[ref], z_sem.at[q]).wait()
     for m in (1, 2, 3):
         pltpu.make_async_copy(last.at[0], last.at[0], s_last).wait()
 
@@ -443,7 +436,7 @@
         exchange,
         out_shape=jax.ShapeDtypeStruct((64, 64, 256), F32),
         in_specs=[pl.BlockSpec(memory_space=pltpu.HBM)] * 6,
-        out_specs=pl.BlockSpec(memory_space=pl.ANY),
+        out_specs=pl.BlockSpec(memory_space=pltpu.VMEM),
         scratch_shapes=[
             pltpu.VMEM((2, 8, 8, 8192), BF16),
             pltpu.VMEM((64, 16, 128), F32),
@@ -456,7 +449,6 @@
             pltpu.VMEM((4096, 128), jnp.int32),
             pltpu.VMEM((512, 256), BF16),
             pltpu.VMEM((512, 256), BF16),
-            pltpu.VMEM((64, 64, 256), F32),
             pltpu.VMEM((16, 64), jnp.int32),
             pltpu.VMEM((16, 64), F32),
             pltpu.SMEM((16, 64), F32),
@@ -465,7 +457,8 @@
             pltpu.VMEM((72, 128), F32),
             pltpu.VMEM((128, 128), F32),
             pltpu.VMEM((2, 4, 8, 2048), BF16),
-            pltpu.VMEM((2, 2, 1, 2048), F32),
+            pltpu.VMEM((2, 2, 1, 2048), BF16),
+            pltpu.VMEM((2, 1, 8192), BF16),
             pltpu.VMEM((2, 8, 8192), F32),
             pltpu.VMEM((2, 1, 2048), F32),
             pltpu.VMEM((1, 8192), F32),
@@ -479,7 +472,6 @@
             dma,
             dma((4,)),
             dma((2,)),
-            dma((CHUNKS,)),
             dma((2,)),
             pltpu.SemaphoreType.REGULAR,
             pltpu.SemaphoreType.REGULAR,

time: 45.3 us -> 45.1 us (level)
  no operation moved by 1% of the time
where the time goes in v3:
time: 45.1 us; the launch traced here: 44.9 us
  Pallas kernels  44.3 us (98%)
  between operations  0.64 us (1%)
    pallas_call x1, Pallas kernels, run_exchange(): pl.pallas_call(exchange, out_shape=jax.ShapeDtypeStruct((64, 64, 256), F3...  41.8 us
    pallas_call x1, Pallas kernels, run_finish(): pl.pallas_call(finish, out_shape=[jax.ShapeDtypeStruct((64, NR), F32)] *...  2.55 us

profile of v3, /device:TPU:1, one launch (start us, length us, event | category | flops | bytes accessed | tf_op | source)
XLA Modules:
  0.0 44.9 jit_solution(18069677585245603411)
XLA Ops:
  0.6 41.8 %exchange.1.z_ref = f32[64,64,256]{2,1,0:T(8,128)S(1)} custom-call(bf16[4,8,8,2048]{3,2,1,0:T(8,128)(2,1)} %bitcast.1, s32[16,64]{1,0:T(8,128)} %exps_in.1, bf16[2,768,256]{2,1,0:T(8,128)(2,1)} %constant.8.clone.send_w, bf16[768,256]{1,0:T(8,128)(2,1)} %constant.9.clone.recv_w, f32[72,128]{1,0:T(8,128)} %constant.10.clone.send_t, ...), custom_call_target="tpu_custom_call" | custom-call | tf_op jit(solution)/shard_map/exchange/pallas_call | solution.py:435
  42.4 2.6 %finish.1 = (f32[64,8192]{1,0:T(8,128)}, f32[64,8192]{1,0:T(8,128)}) custom-call(f32[64,64,256]{2,1,0:T(8,128)S(1)} %exchange.1.z_ref), custom_call_target="tpu_custom_call" | custom-call | tf_op jit(solution)/shard_map/finish/pallas_call | solution.py:522

commit v4 on v3

--- a/solution.py
+++ b/solution.py
@@ -13,7 +13,7 @@
 NC = 8192
 MESH = pl.DeviceIdType.MESH
 CHUNKS = 8
-LAG = 4
+LAG = 3
 TOP = 32767.0
 BOUND = 16896.0
 DECODED = BOUND / TOP**4

time: 45.1 us -> 45.1 us (level)
  no operation moved by 1% of the time
where the time goes in v4:
time: 45.1 us; the launch traced here: 44.9 us
  Pallas kernels  44.3 us (98%)
  between operations  0.64 us (1%)
    pallas_call x1, Pallas kernels, run_exchange(): pl.pallas_call(exchange, out_shape=jax.ShapeDtypeStruct((64, 64, 256), F3...  41.8 us
    pallas_call x1, Pallas kernels, run_finish(): pl.pallas_call(finish, out_shape=[jax.ShapeDtypeStruct((64, NR), F32)] *...  2.55 us

profile of v4, /device:TPU:1, one launch (start us, length us, event | category | flops | bytes accessed | tf_op | source)
XLA Modules:
  0.0 44.9 jit_solution(2550491057627112008)
XLA Ops:
  0.6 41.8 %exchange.1.z_ref = f32[64,64,256]{2,1,0:T(8,128)S(1)} custom-call(bf16[4,8,8,2048]{3,2,1,0:T(8,128)(2,1)} %bitcast.1, s32[16,64]{1,0:T(8,128)} %exps_in.1, bf16[2,768,256]{2,1,0:T(8,128)(2,1)} %constant.8.clone.send_w, bf16[768,256]{1,0:T(8,128)(2,1)} %constant.9.clone.recv_w, f32[72,128]{1,0:T(8,128)} %constant.10.clone.send_t, ...), custom_call_target="tpu_custom_call" | custom-call | tf_op jit(solution)/shard_map/exchange/pallas_call | solution.py:435
  42.4 2.6 %finish.1 = (f32[64,8192]{1,0:T(8,128)}, f32[64,8192]{1,0:T(8,128)}) custom-call(f32[64,64,256]{2,1,0:T(8,128)S(1)} %exchange.1.z_ref), custom_call_target="tpu_custom_call" | custom-call | tf_op jit(solution)/shard_map/finish/pallas_call | solution.py:522
